TPU v7x, 128 devices: a whole 4x4x4 slice. The times are simulated.
128 devices in a mesh: gx: 4 (over x), gz: 4 (over y_lo, core), ta: 8 (over z, y_hi).
Axes of the slice: x: 4, y: 4 (y_hi: 2, y_lo: 2; y = y_hi * 2 + y_lo), z: 4, core: 2. Of those that a mesh axis runs over, the one named last changes fastest.
Arguments:
- propagator: float32 [2, 12, 12, 1048576], P(None, None, None, ('gx', 'gz', 'ta')), may hold values from -6 to 6
- momenta: int32 [512, 4], P(('gx', 'gz', 'ta')), may hold values from -16 to 15
- gamma_index: int32 [16], replicated, may hold values from 0 to 15, each once
Outputs:
- vertices: float32 [512, 16, 2, 12, 12], P(('gx', 'gz', 'ta'))
Inputs may be any that keep to these rules, and one draw needn't show every extreme that they name: `momenta`: A momentum component enters only modulo the lattice length along its direction. `gamma_index`: every mask of 0 to 15 appears once.
All inputs are finite; a program needn't handle non-finite values.
Results may differ from a plain program's by a relative error of at most 0.0001.
Values sent between devices are 32-bit elements; how exact they have to be, the bound alone decides.
A program may use at most 128 MiB of HBM per device.

v0:
```python
import math
import jax
import jax.numpy as jnp
import numpy as np
from jax import lax
from jax.sharding import PartitionSpec as P

LX = 32
LY = 32
LZ = 32
LT = 32


def in_blocks(array, dim, devices):
    before, after = (array.shape[:dim], array.shape[dim + 1 :])
    return jnp.moveaxis(array.reshape(*before, devices, -1, *after), dim, 0)


def summed_on_arrival(array, axis, dim):
    devices = lax.axis_size(axis)
    blocks = lax.all_to_all(in_blocks(array, dim, devices), axis, 0, 0, tiled=True)
    return jnp.sum(blocks, axis=0)


def clifford_table():
    zeros = np.zeros((4, 4))
    first = (zeros, np.array([[0, 0, 0, 1], [0, 0, 1, 0], [0, -1, 0, 0], [-1, 0, 0, 0]]))
    second = (np.array([[0, 0, 0, -1], [0, 0, 1, 0], [0, 1, 0, 0], [-1, 0, 0, 0]]), zeros)
    third = (zeros, np.array([[0, 0, 1, 0], [0, 0, 0, -1], [-1, 0, 0, 0], [0, 1, 0, 0]]))
    fourth = (np.array([[0, 0, 1, 0], [0, 0, 0, 1], [1, 0, 0, 0], [0, 1, 0, 0]]), zeros)
    basis = [first, second, third, fourth]
    tables_re = []
    tables_im = []
    for mask in range(16):
        matrix_re = np.identity(4)
        matrix_im = np.zeros((4, 4))
        for bit in range(4):
            if mask >> bit & 1:
                basis_re, basis_im = basis[bit]
                new_re = matrix_re @ basis_re - matrix_im @ basis_im
                new_im = matrix_re @ basis_im + matrix_im @ basis_re
                matrix_re, matrix_im = (new_re, new_im)
        tables_re.append(matrix_re)
        tables_im.append(matrix_im)
    return (np.stack(tables_re), np.stack(tables_im))


def select_gammas(gamma_index):
    table_re, table_im = clifford_table()
    onehot = (gamma_index[:, None] == jnp.arange(16, dtype=jnp.int32)[None, :]).astype(jnp.float32)
    high = lax.Precision.HIGHEST
    chosen_re = jnp.einsum(
        "gk,kst->gst", onehot, jnp.asarray(table_re, jnp.float32), precision=high
    )
    chosen_im = jnp.einsum(
        "gk,kst->gst", onehot, jnp.asarray(table_im, jnp.float32), precision=high
    )
    return (chosen_re, chosen_im)


def vertices_of(spec_re, spec_im, gamma_re, gamma_im):
    high = lax.Precision.HIGHEST
    count = spec_re.shape[0]
    split_re = spec_re.reshape(count, 4, 3, 12)
    split_im = spec_im.reshape(count, 4, 3, 12)
    turned_re = (
        jnp.einsum("gst,mtcb->mgscb", gamma_re, split_re, precision=high)
        - jnp.einsum("gst,mtcb->mgscb", gamma_im, split_im, precision=high)
    ).reshape(count, 16, 12, 12)
    turned_im = (
        jnp.einsum("gst,mtcb->mgscb", gamma_re, split_im, precision=high)
        + jnp.einsum("gst,mtcb->mgscb", gamma_im, split_re, precision=high)
    ).reshape(count, 16, 12, 12)
    result_re = jnp.einsum("mka,mgkb->mgab", spec_re, turned_re, precision=high) + jnp.einsum(
        "mka,mgkb->mgab", spec_im, turned_im, precision=high
    )
    result_im = jnp.einsum("mka,mgkb->mgab", spec_re, turned_im, precision=high) - jnp.einsum(
        "mka,mgkb->mgab", spec_im, turned_re, precision=high
    )
    return jnp.stack([result_re, result_im], axis=2)


def site_coordinates(local_sites):
    block_x = LX // lax.axis_size("gx")
    block_z = LZ // lax.axis_size("gz")
    block_t = LT // lax.axis_size("ta")
    linear = jnp.arange(local_sites, dtype=jnp.int32)
    coord_t = linear % block_t + lax.axis_index("ta") * block_t
    coord_z = linear // block_t % block_z + lax.axis_index("gz") * block_z
    coord_y = linear // (block_t * block_z) % LY
    coord_x = linear // (block_t * block_z * LY) + lax.axis_index("gx") * block_x
    return jnp.stack([coord_x, coord_y, coord_z, coord_t])


def make_term(momentum_rows, coords, plain_re, diff_part, summed_part):
    lengths = (LX, LY, LZ, LT)
    common = lengths[0]
    for length in lengths[1:]:
        common = common * length // math.gcd(common, length)
    high = lax.Precision.HIGHEST

    def single_block(waves):
        phase_index = jnp.zeros((waves.shape[0], coords.shape[1]), jnp.int32)
        for direction in range(4):
            reduced = waves[:, direction] % lengths[direction] * (common // lengths[direction])
            phase_index = phase_index + reduced[:, None] * coords[direction][None, :]
        phase_index = phase_index % common
        angle = phase_index.astype(jnp.float32) * (2.0 * math.pi / float(common))
        cosine = jnp.cos(angle)
        sine = jnp.sin(angle)
        first = jnp.einsum("ms,cs->mc", cosine - sine, plain_re, precision=high)
        second = jnp.einsum("ms,cs->mc", cosine, diff_part, precision=high)
        third = jnp.einsum("ms,cs->mc", -sine, summed_part, precision=high)
        return jnp.concatenate([first - third, first + second], axis=1)

    def term(start, count):
        width = math.gcd(count, 512)
        picked = momentum_rows
        picked = picked.reshape(count // width, width, 4)
        return lax.map(single_block, picked).reshape(count, 288)

    return term


def body(propagator, momenta, gamma_index):
    local_sites = propagator.shape[3]
    mine = momenta.shape[0]
    coords = site_coordinates(local_sites)
    plain_re = propagator[0].reshape(144, local_sites)
    plain_im = propagator[1].reshape(144, local_sites)
    diff_part = plain_im - plain_re
    summed_part = plain_re + plain_im
    gathered = lax.all_gather(momenta, ("gx", "gz", "ta"), axis=0, tiled=True)
    spatial = lax.axis_size("gx") * lax.axis_size("gz")
    ordered = gathered.reshape(spatial, lax.axis_size("ta"), mine, 4)
    ordered = jnp.transpose(ordered, (1, 0, 2, 3)).reshape(-1, 4)
    term = make_term(ordered, coords, plain_re, diff_part, summed_part)
    partial_value = summed_on_arrival(
        term(jnp.int32(0), spatial * mine * lax.axis_size("ta")), "ta", 0
    )
    spectrum = summed_on_arrival(partial_value, ("gx", "gz"), 0)
    spectrum = spectrum * (1.0 / math.sqrt(float(LX * LY * LZ * LT)))
    spectrum = spectrum.reshape(mine, 2, 12, 12)
    gamma_re, gamma_im = select_gammas(gamma_index)
    return vertices_of(spectrum[:, 0], spectrum[:, 1], gamma_re, gamma_im)


def solution(mesh):
    placed = (P(None, None, None, ("gx", "gz", "ta")), P(("gx", "gz", "ta"), None), P())
    return jax.shard_map(
        body,
        mesh=mesh,
        in_specs=placed,
        out_specs=P(("gx", "gz", "ta"), None, None, None, None),
        check_vma=False,
    )
```

profile of v0, /device:TPU:1, one launch (start us, length us, event | category | flops | bytes accessed | tf_op | source)
XLA Modules:
  0.0 679.2 jit_solution(13706072542922024557)
XLA Ops:
  0.0 32.7 %slice_reduce_fusion = (f32[12,12,8192]{2,1,0:T(8,128)}, f32[12,12,8192]{2,1,0:T(8,128)}) fusion(f32[2,12,12,8192]{3,0,2,1:T(2,128)} %param.5), kind=kLoop, calls=%fused_computation.15 | loop fusion | bytes 18874368 | tf_op jit(solution)/shard_map/slice | solution.py:130
  32.7 6.0 reshape_squeeze.12
  38.7 6.0 reshape_squeeze.13
  44.7 6.9 %fusion.108 = f32[144,8192]{1,0:T(8,128)} fusion(f32[144,8192]{1,0:T(8,128)} %reshape_squeeze.13, f32[144,8192]{1,0:T(8,128)} %reshape_squeeze.12), kind=kLoop, calls=%fused_computation.13.clone.clone.clone.2 | loop fusion | flops 1179648 | bytes 14155776 | tf_op jit(solution)/shard_map/while/body/eval_jaxpr/ms,cs->mc/dot_general | solution.py:112
  51.6 0.0 slice-done
  51.6 0.0 slice-done.1
  51.6 1.2 copy-done
  52.8 3.0 fusion.110
  55.8 0.0 copy-done.1
  55.8 310.6 %all-gather = s32[128,4,4]{2,1,0:T(4,128)S(1)} all-gather(s32[1,4,4]{2,1,0:T(4,128)S(1)} %bitcast.115), channel_id=1, replica_groups=mesh['gx'=4,'gz'=4,'ta'=8] {'gx','gz','ta'}, dimensions={0}, use_global_device_ids=true | all-gather | bytes 8256 | tf_op jit(solution)/shard_map/all_gather | solution.py:133
  366.4 1.0 copy.58
  367.4 0.2 squeeze.19
  367.7 0.0 slice-start.3
  367.7 0.0 slice-start.6
  367.7 72.3 %fusion.106 = f32[512,8192]{1,0:T(8,128)} fusion(s32[8192]{0:T(1024)S(1)} %get-tuple-element.46, s32[512]{0:T(512)S(1)} %bitcast.106, s32[8192]{0:T(1024)S(1)} %get-tuple-element.45, s32[512]{0:T(512)S(1)} %bitcast.109, s32[8192]{0:T(1024)S(1)} %get-tuple-element.42, s32[512]{0:T(512)S(1)} %bitcast.112, s32[8192]{0:T(1024)S(1)} %get-tuple-element.44, ...), kind=kLoop, calls=%fused_computation.9.clone.1 | loop fusion | flops 88080384 | bytes 16916480 | tf_op jit(solution)/shard_map/while/body/eval_jaxpr/ms,cs->mc/dot_general | solution.py:111
  440.0 0.0 slice-done.2
  440.0 0.0 slice-start.7
  440.0 0.0 slice-start.4
  440.0 20.4 %fusion.5 = f32[512,144]{0,1:T(8,128)S(1)} fusion(f32[144,8192]{1,0:T(8,128)S(1)} %bitcast.86, f32[512,8192]{1,0:T(8,128)} %fusion.106), kind=kOutput, calls=%fused_computation.8 | convolution fusion | flops 7247757312 | bytes 21790720 | tf_op jit(solution)/shard_map/while/body/eval_jaxpr/ms,cs->mc/dot_general | solution.py:111
  460.5 0.0 slice-start.5
  460.5 80.0 %fusion.20 = f32[512,144]{0,1:T(8,128)S(1)} fusion(f32[512,144]{0,1:T(8,128)S(1)} %fusion.5, s32[8192]{0:T(1024)S(1)} %get-tuple-element.46, s32[512]{0:T(512)S(1)} %bitcast.107, s32[8192]{0:T(1024)S(1)} %get-tuple-element.45, s32[512]{0:T(512)S(1)} %bitcast.110, s32[8192]{0:T(1024)S(1)} %get-tuple-element.42, s32[512]{0:T(512)S(1)} %bitcast.113, ...), kind=kOutput, calls=%fused_computation.25 | convolution fusion | flops 7331717120 | bytes 5447680 | tf_op jit(solution)/shard_map/while/body/eval_jaxpr/ms,cs->mc/dot_general | solution.py:112
  540.5 0.0 copy-start.2
  540.5 0.0 copy-start.4
  540.6 0.0 copy-start.3
  540.6 94.9 %fusion.25 = f32[512,144]{0,1:T(8,128)S(1)} fusion(f32[512,144]{0,1:T(8,128)S(1)} %fusion.5, s32[8192]{0:T(1024)S(1)} %get-tuple-element.46, s32[512]{0:T(512)S(1)} %bitcast.108, s32[8192]{0:T(1024)S(1)} %get-tuple-element.45, s32[512]{0:T(512)S(1)} %bitcast.111, s32[8192]{0:T(1024)S(1)} %get-tuple-element.42, s32[512]{0:T(512)S(1)} %bitcast.114, ...), kind=kOutput, calls=%fused_computation.26 | convolution fusion | flops 7335911424 | bytes 5447680 | tf_op jit(solution)/shard_map/while/body/eval_jaxpr/ms,cs->mc/dot_general | solution.py:113
  635.5 1.2 copy.59
  636.7 3.5 all-to-all-start
  640.2 0.2 fusion.61
  640.4 10.2 %all-to-all-done = f32[8,64,288]{2,1,0:T(8,128)S(1)} async-done(((f32[8,64,288]{2,1,0:T(8,128)}), f32[8,64,288]{2,1,0:T(8,128)S(1)}, u32[]{:S(2)}, u32[]{:S(2)}) %all-to-all-start) | async-done | bytes 589856 | tf_op jit(solution)/shard_map/all_to_all | solution.py:21
  650.6 0.7 reshape.89
  651.3 14.7 %all-to-all-start.1 = ((f32[16,4,288]{2,1,0:T(4,128)}), f32[16,4,288]{2,1,0:T(4,128)S(1)}, u32[]{:S(2)}, u32[]{:S(2)}) async-start(f32[16,4,288]{2,1,0:T(4,128)} %reshape.89), calls=%async_computation.1 | async-start | bytes 196608 | tf_op jit(solution)/shard_map/all_to_all | solution.py:21
  666.0 0.2 fusion.60
  666.2 5.8 all-to-all-done.1
  672.0 0.1 mul.133
  672.2 0.6 fusion.54
  672.7 0.6 fusion.58
  673.3 0.6 fusion.18
  673.9 0.2 copy.71
  674.1 0.4 copy.72
  674.4 0.5 fusion.46
  674.9 0.6 fusion.19
  675.5 0.2 copy.67
  675.7 0.4 copy.68
  676.0 0.5 fusion.48
  676.5 0.5 fusion.16
  677.0 0.5 fusion.17
  677.4 0.1 pad_maximum_fusion
  677.5 1.5 copy.75
  (27 shorter events, 0.2 us)
Async XLA Ops:
  38.7 12.9 %slice-start = ((s8[4718592]{0:T(1024)(128)(4,1)}), s8[524288]{0:T(1024)(128)(4,1)S(1)}, s32[]{:S(2)}) async-start(s8[4718592]{0:T(1024)(128)(4,1)} %bitcast.83), calls=%async_computation.2 | async-start | bytes 1048576
  44.7 6.9 %slice-start.1 = ((s8[4718592]{0:T(1024)(128)(4,1)}), s8[4194304]{0:T(1024)(128)(4,1)S(1)}, s32[]{:S(2)}) async-start(s8[4718592]{0:T(1024)(128)(4,1)} %bitcast.83), calls=%async_computation.3 | async-start | bytes 8388608
  44.7 8.1 %copy-start = (f32[144,8192]{1,0:T(8,128)S(1)}, f32[144,8192]{1,0:T(8,128)}, u32[]{:S(2)}) copy-start(f32[144,8192]{1,0:T(8,128)} %reshape_squeeze.13) | copy-start | bytes 14155780
  44.7 11.1 %copy-start.1 = (s32[4,4]{1,0:T(4,128)S(1)}, s32[4,4]{1,0:T(4,128)}, u32[]{:S(2)}) copy-start(s32[4,4]{1,0:T(4,128)} %param.6) | copy-start | bytes 196
  52.8 387.2 %slice-start.2 = ((s8[4718592]{0:T(1024)(128)(4,1)}), s8[524288]{0:T(1024)(128)(4,1)S(1)}, s32[]{:S(2)}) async-start(s8[4718592]{0:T(1024)(128)(4,1)} %bitcast.85), calls=%async_computation.4 | async-start | bytes 1048576
  367.7 72.3 %slice-start.3 = ((s8[4718592]{0:T(1024)(128)(4,1)}), s8[4194304]{0:T(1024)(128)(4,1)S(1)}, s32[]{:S(2)}) async-start(s8[4718592]{0:T(1024)(128)(4,1)} %bitcast.85), calls=%async_computation.5 | async-start | bytes 8388608
  367.7 92.8 %slice-start.6 = ((s8[4718592]{0:T(1024)(128)(4,1)}), s8[4194304]{0:T(1024)(128)(4,1)S(1)}, s32[]{:S(2)}) async-start(s8[4718592]{0:T(1024)(128)(4,1)} %bitcast.89), calls=%async_computation.8 | async-start | bytes 8388608
  440.0 20.5 %slice-start.7 = ((s8[4718592]{0:T(1024)(128)(4,1)}), s8[524288]{0:T(1024)(128)(4,1)S(1)}, s32[]{:S(2)}) async-start(s8[4718592]{0:T(1024)(128)(4,1)} %bitcast.89), calls=%async_computation.9 | async-start | bytes 1048576
  440.0 100.5 %slice-start.4 = ((s8[4718592]{0:T(1024)(128)(4,1)}), s8[524288]{0:T(1024)(128)(4,1)S(1)}, s32[]{:S(2)}) async-start(s8[4718592]{0:T(1024)(128)(4,1)} %bitcast.87), calls=%async_computation.6 | async-start | bytes 1048576
  460.5 80.0 %slice-start.5 = ((s8[4718592]{0:T(1024)(128)(4,1)}), s8[4194304]{0:T(1024)(128)(4,1)S(1)}, s32[]{:S(2)}) async-start(s8[4718592]{0:T(1024)(128)(4,1)} %bitcast.87), calls=%async_computation.7 | async-start | bytes 8388608
  540.5 99.7 %copy-start.2 = (s32[16]{0:T(128)S(1)}, s32[16]{0:T(128)}, u32[]{:S(2)}) copy-start(s32[16]{0:T(128)} %param.7) | copy-start | bytes 196
  540.5 99.7 %copy-start.4 = (f32[16,16]{0,1:T(8,128)S(1)}, f32[16,16]{0,1:T(8,128)}, u32[]{:S(2)}) copy-start(f32[16,16]{0,1:T(8,128)} %constant.146) | copy-start | bytes 3076
  540.6 125.4 %copy-start.3 = (f32[16,16]{0,1:T(8,128)S(1)}, f32[16,16]{0,1:T(8,128)}, u32[]{:S(2)}) copy-start(f32[16,16]{0,1:T(8,128)} %constant.147) | copy-start | bytes 3076
  636.7 13.9 %all-to-all-start = ((f32[8,64,288]{2,1,0:T(8,128)}), f32[8,64,288]{2,1,0:T(8,128)S(1)}, u32[]{:S(2)}, u32[]{:S(2)}) async-start(f32[8,64,288]{2,1,0:T(8,128)} %bitcast.7), calls=%async_computation | async-start | bytes 1572864 | tf_op jit(solution)/shard_map/all_to_all | solution.py:21
  651.3 20.6 %all-to-all-start.1 = ((f32[16,4,288]{2,1,0:T(4,128)}), f32[16,4,288]{2,1,0:T(4,128)S(1)}, u32[]{:S(2)}, u32[]{:S(2)}) async-start(f32[16,4,288]{2,1,0:T(4,128)} %reshape.89), calls=%async_computation.1 | async-start | bytes 196608 | tf_op jit(solution)/shard_map/all_to_all | solution.py:21
where the time goes:
time: 684 us; the launch traced here: 679 us
  blocking collectives  311 us (45%)
  matrix products  200 us (29%)
  other arithmetic  82.4 us (12%)
  local copies, waits for them, and re-layouts  51.7 us (8%)
  starting transfers between devices  18.2 us (3%)
  waiting for transfers between devices  15.9 us (2%)
    all_gather x1, blocking collectives, body(): gathered = lax.all_gather(momenta, ('gx', 'gz', 'ta'), axis=0, tiled=True)  311 us
    dot_general x1, matrix products, single_block(): third = jnp.einsum('ms,cs->mc', -sine, summed_part, precision=high)  94.9 us
    dot_general x1, matrix products, single_block(): second = jnp.einsum('ms,cs->mc', cosine, diff_part, precision=high)  80 us
    dot_general x1, other arithmetic, single_block(): first = jnp.einsum('ms,cs->mc', cosine - sine, plain_re, precision=high)  72.3 us
    slice x1, local copies, waits for them, and re-layouts, body(): plain_im = propagator[1].reshape(144, local_sites)  32.7 us
    dot_general x1, matrix products, single_block(): first = jnp.einsum('ms,cs->mc', cosine - sine, plain_re, precision=high)  20.4 us
    all_to_all x2, starting transfers between devices, summed_on_arrival(): lax.all_to_all(in_blocks(array, dim, devices), axis, 0, 0, tiled=True)  18.2 us
    all_to_all x2, waiting for transfers between devices, summed_on_arrival(): lax.all_to_all(in_blocks(array, dim, devices), axis, 0, 0, tiled=True)  15.9 us
  transfers between devices with their start and end apart: 2, of which 2 were waited for; matrix products, arithmetic and copies ran while one was open for 0% of the time, Pallas kernels for 0%

commit v1 on v0

--- a/solution.py
+++ b/solution.py
@@ -130,7 +130,10 @@
     plain_im = propagator[1].reshape(144, local_sites)
     diff_part = plain_im - plain_re
     summed_part = plain_re + plain_im
-    gathered = lax.all_gather(momenta, ("gx", "gz", "ta"), axis=0, tiled=True)
+    size = lax.axis_size(("gx", "gz", "ta"))
+    tiles = jnp.stack([momenta for _ in range(size)])
+    tiles = lax.all_to_all(tiles, ("gx", "gz", "ta"), split_axis=0, concat_axis=0)
+    gathered = jnp.concatenate(tiles, axis=0)
     spatial = lax.axis_size("gx") * lax.axis_size("gz")
     ordered = gathered.reshape(spatial, lax.axis_size("ta"), mine, 4)
     ordered = jnp.transpose(ordered, (1, 0, 2, 3)).reshape(-1, 4)

time: 684 us -> 385 us (0.56)
  blocking collectives: 311 us -> 0 us
    all_gather x1 -> x0, blocking collectives: 311 us -> none  [body(): gathered = lax.all_gather(momenta, ('gx', 'gz', 'ta'), axis=0, tiled=True)]
    all_to_all x0 -> x1, starting transfers between devices: none -> 11.5 us  [body(): lax.all_to_all(tiles, ('gx', 'gz', 'ta'), split_axis=0, concat_axis=0)]
  transfers between devices with their start and end apart: 2 -> 3, of which waited for: 2 -> 2; matrix products, arithmetic and copies ran while one was open for 0% -> 14% of each run, Pallas kernels for 0% -> 0%
where the time goes in v1:
time: 385 us; the launch traced here: 379 us
  matrix products  200 us (52%)
  other arithmetic  82.3 us (21%)
  local copies, waits for them, and re-layouts  53.1 us (14%)
  starting transfers between devices  24.7 us (6%)
  waiting for transfers between devices  19.1 us (5%)
    dot_general x1, matrix products, single_block(): third = jnp.einsum('ms,cs->mc', -sine, summed_part, precision=high)  94.8 us
    dot_general x1, matrix products, single_block(): second = jnp.einsum('ms,cs->mc', cosine, diff_part, precision=high)  79.9 us
    dot_general x1, other arithmetic, single_block(): first = jnp.einsum('ms,cs->mc', cosine - sine, plain_re, precision=high)  72.2 us
    slice x1, local copies, waits for them, and re-layouts, body(): plain_im = propagator[1].reshape(144, local_sites)  32.7 us
    dot_general x1, matrix products, single_block(): first = jnp.einsum('ms,cs->mc', cosine - sine, plain_re, precision=high)  20.4 us
    all_to_all x2, waiting for transfers between devices, summed_on_arrival(): lax.all_to_all(in_blocks(array, dim, devices), axis, 0, 0, tiled=True)  19.1 us
    all_to_all x2, starting transfers between devices, summed_on_arrival(): lax.all_to_all(in_blocks(array, dim, devices), axis, 0, 0, tiled=True)  13.2 us
    all_to_all x1, starting transfers between devices, body(): lax.all_to_all(tiles, ('gx', 'gz', 'ta'), split_axis=0, concat_axis=0)  11.5 us
  transfers between devices with their start and end apart: 3, of which 2 were waited for; matrix products, arithmetic and copies ran while one was open for 14% of the time, Pallas kernels for 0%

profile of v1, /device:TPU:1, one launch (start us, length us, event | category | flops | bytes accessed | tf_op | source)
XLA Modules:
  0.0 379.4 jit_solution(7399322305674453684)
XLA Ops:
  0.0 1.4 stack.8
  1.4 11.5 %all-to-all-start = ((s32[128,4,4]{2,1,0:T(4,128)}), s32[128,4,4]{2,1,0:T(4,128)S(1)}, u32[]{:S(2)}, u32[]{:S(2)}) async-start(s32[128,4,4]{2,1,0:T(4,128)} %stack.8), calls=%async_computation | async-start | bytes 524288 | tf_op jit(solution)/shard_map/all_to_all | solution.py:135
  12.9 32.7 %slice_reduce_fusion = (f32[12,12,8192]{2,1,0:T(8,128)}, f32[12,12,8192]{2,1,0:T(8,128)}) fusion(f32[2,12,12,8192]{3,0,2,1:T(2,128)} %param.5), kind=kLoop, calls=%fused_computation.15 | loop fusion | bytes 18874368 | tf_op jit(solution)/shard_map/slice | solution.py:130
  45.6 6.0 %reshape_squeeze.12 = f32[144,8192]{1,0:T(8,128)} reshape(f32[12,12,8192]{2,1,0:T(8,128)} %get-tuple-element.24) | data formatting | bytes 9437184 | tf_op jit(solution)/shard_map/reshape;squeeze | solution.py:129
  51.6 6.0 %reshape_squeeze.13 = f32[144,8192]{1,0:T(8,128)} reshape(f32[12,12,8192]{2,1,0:T(8,128)} %get-tuple-element.23) | data formatting | bytes 9437184 | tf_op jit(solution)/shard_map/reshape;squeeze | solution.py:130
  57.6 6.9 %fusion.108 = f32[144,8192]{1,0:T(8,128)} fusion(f32[144,8192]{1,0:T(8,128)} %reshape_squeeze.13, f32[144,8192]{1,0:T(8,128)} %reshape_squeeze.12), kind=kLoop, calls=%fused_computation.13.clone.clone.clone.2 | loop fusion | flops 1179648 | bytes 14155776 | tf_op jit(solution)/shard_map/while/body/eval_jaxpr/ms,cs->mc/dot_general | solution.py:112
  64.5 0.0 slice-done
  64.5 1.2 copy-done
  65.7 3.0 fusion.110
  68.7 0.0 all-to-all-done
  68.7 1.0 copy.104
  69.7 0.2 squeeze.19
  70.0 0.0 slice-start.3
  70.0 0.0 slice-start.6
  70.0 72.2 %fusion.106 = f32[512,8192]{1,0:T(8,128)} fusion(s32[8192]{0:T(1024)S(1)} %get-tuple-element.46, s32[512]{0:T(512)S(1)} %bitcast.106, s32[8192]{0:T(1024)S(1)} %get-tuple-element.45, s32[512]{0:T(512)S(1)} %bitcast.109, s32[8192]{0:T(1024)S(1)} %get-tuple-element.42, s32[512]{0:T(512)S(1)} %bitcast.112, s32[8192]{0:T(1024)S(1)} %get-tuple-element.44, ...), kind=kLoop, calls=%fused_computation.9.clone.1 | loop fusion | flops 88080384 | bytes 16916480 | tf_op jit(solution)/shard_map/while/body/eval_jaxpr/ms,cs->mc/dot_general | solution.py:111
  142.2 0.0 slice-done.2
  142.2 0.0 slice-start.7
  142.2 0.0 slice-start.4
  142.2 20.4 %fusion.5 = f32[512,144]{0,1:T(8,128)S(1)} fusion(f32[144,8192]{1,0:T(8,128)S(1)} %bitcast.86, f32[512,8192]{1,0:T(8,128)} %fusion.106), kind=kOutput, calls=%fused_computation.8 | convolution fusion | flops 7247757312 | bytes 21790720 | tf_op jit(solution)/shard_map/while/body/eval_jaxpr/ms,cs->mc/dot_general | solution.py:111
  162.7 0.0 slice-start.5
  162.7 79.9 %fusion.20 = f32[512,144]{0,1:T(8,128)S(1)} fusion(f32[512,144]{0,1:T(8,128)S(1)} %fusion.5, s32[8192]{0:T(1024)S(1)} %get-tuple-element.46, s32[512]{0:T(512)S(1)} %bitcast.107, s32[8192]{0:T(1024)S(1)} %get-tuple-element.45, s32[512]{0:T(512)S(1)} %bitcast.110, s32[8192]{0:T(1024)S(1)} %get-tuple-element.42, s32[512]{0:T(512)S(1)} %bitcast.113, ...), kind=kOutput, calls=%fused_computation.25 | convolution fusion | flops 7331717120 | bytes 5447680 | tf_op jit(solution)/shard_map/while/body/eval_jaxpr/ms,cs->mc/dot_general | solution.py:112
  242.7 0.0 copy-start.1
  242.7 0.0 copy-start.3
  242.7 0.0 copy-start.2
  242.7 94.8 %fusion.25 = f32[512,144]{0,1:T(8,128)S(1)} fusion(f32[512,144]{0,1:T(8,128)S(1)} %fusion.5, s32[8192]{0:T(1024)S(1)} %get-tuple-element.46, s32[512]{0:T(512)S(1)} %bitcast.108, s32[8192]{0:T(1024)S(1)} %get-tuple-element.45, s32[512]{0:T(512)S(1)} %bitcast.111, s32[8192]{0:T(1024)S(1)} %get-tuple-element.42, s32[512]{0:T(512)S(1)} %bitcast.114, ...), kind=kOutput, calls=%fused_computation.26 | convolution fusion | flops 7335911424 | bytes 5447680 | tf_op jit(solution)/shard_map/while/body/eval_jaxpr/ms,cs->mc/dot_general | solution.py:113
  337.6 1.2 copy.78
  338.7 7.1 %all-to-all-start.1 = ((f32[8,64,288]{2,1,0:T(8,128)}), f32[8,64,288]{2,1,0:T(8,128)S(1)}, u32[]{:S(2)}, u32[]{:S(2)}) async-start(f32[8,64,288]{2,1,0:T(8,128)} %bitcast.7), calls=%async_computation.1 | async-start | bytes 1572864 | tf_op jit(solution)/shard_map/all_to_all | solution.py:21
  345.8 0.2 fusion.61
  346.0 13.3 %all-to-all-done.1 = f32[8,64,288]{2,1,0:T(8,128)S(1)} async-done(((f32[8,64,288]{2,1,0:T(8,128)}), f32[8,64,288]{2,1,0:T(8,128)S(1)}, u32[]{:S(2)}, u32[]{:S(2)}) %all-to-all-start.1) | async-done | bytes 589856 | tf_op jit(solution)/shard_map/all_to_all | solution.py:21
  359.4 0.7 reshape.87
  360.1 6.2 %all-to-all-start.2 = ((f32[16,4,288]{2,1,0:T(4,128)}), f32[16,4,288]{2,1,0:T(4,128)S(1)}, u32[]{:S(2)}, u32[]{:S(2)}) async-start(f32[16,4,288]{2,1,0:T(4,128)} %reshape.87), calls=%async_computation.2 | async-start | bytes 196608 | tf_op jit(solution)/shard_map/all_to_all | solution.py:21
  366.2 0.2 fusion.60
  366.4 5.7 %all-to-all-done.2 = f32[16,4,288]{2,1,0:T(4,128)S(1)} async-done(((f32[16,4,288]{2,1,0:T(4,128)}), f32[16,4,288]{2,1,0:T(4,128)S(1)}, u32[]{:S(2)}, u32[]{:S(2)}) %all-to-all-start.2) | async-done | bytes 73760 | tf_op jit(solution)/shard_map/all_to_all | solution.py:21
  372.2 0.1 mul.133
  372.3 0.6 fusion.54
  372.9 0.6 fusion.58
  373.5 0.6 fusion.18
  374.1 0.2 copy.90
  374.3 0.4 copy.91
  374.6 0.5 fusion.46
  375.1 0.6 fusion.19
  375.7 0.2 copy.86
  375.9 0.4 copy.87
  376.2 0.5 fusion.48
  376.7 0.5 fusion.16
  377.2 0.5 fusion.17
  377.6 0.1 pad_maximum_fusion
  377.7 1.5 copy.94
  (27 shorter events, 0.2 us)
Async XLA Ops:
  1.4 67.3 %all-to-all-start = ((s32[128,4,4]{2,1,0:T(4,128)}), s32[128,4,4]{2,1,0:T(4,128)S(1)}, u32[]{:S(2)}, u32[]{:S(2)}) async-start(s32[128,4,4]{2,1,0:T(4,128)} %stack.8), calls=%async_computation | async-start | bytes 524288 | tf_op jit(solution)/shard_map/all_to_all | solution.py:135
  51.6 12.9 %slice-start = ((s8[4718592]{0:T(1024)(128)(4,1)}), s8[524288]{0:T(1024)(128)(4,1)S(1)}, s32[]{:S(2)}) async-start(s8[4718592]{0:T(1024)(128)(4,1)} %bitcast.83), calls=%async_computation.3 | async-start | bytes 1048576
  57.6 6.9 %slice-start.1 = ((s8[4718592]{0:T(1024)(128)(4,1)}), s8[4194304]{0:T(1024)(128)(4,1)S(1)}, s32[]{:S(2)}) async-start(s8[4718592]{0:T(1024)(128)(4,1)} %bitcast.83), calls=%async_computation.4 | async-start | bytes 8388608
  57.6 8.1 %copy-start = (f32[144,8192]{1,0:T(8,128)S(1)}, f32[144,8192]{1,0:T(8,128)}, u32[]{:S(2)}) copy-start(f32[144,8192]{1,0:T(8,128)} %reshape_squeeze.13) | copy-start | bytes 14155780
  65.7 76.5 %slice-start.2 = ((s8[4718592]{0:T(1024)(128)(4,1)}), s8[524288]{0:T(1024)(128)(4,1)S(1)}, s32[]{:S(2)}) async-start(s8[4718592]{0:T(1024)(128)(4,1)} %bitcast.85), calls=%async_computation.5 | async-start | bytes 1048576
  70.0 72.2 %slice-start.3 = ((s8[4718592]{0:T(1024)(128)(4,1)}), s8[4194304]{0:T(1024)(128)(4,1)S(1)}, s32[]{:S(2)}) async-start(s8[4718592]{0:T(1024)(128)(4,1)} %bitcast.85), calls=%async_computation.6 | async-start | bytes 8388608
  70.0 92.7 %slice-start.6 = ((s8[4718592]{0:T(1024)(128)(4,1)}), s8[4194304]{0:T(1024)(128)(4,1)S(1)}, s32[]{:S(2)}) async-start(s8[4718592]{0:T(1024)(128)(4,1)} %bitcast.89), calls=%async_computation.9 | async-start | bytes 8388608
  142.2 20.5 %slice-start.7 = ((s8[4718592]{0:T(1024)(128)(4,1)}), s8[524288]{0:T(1024)(128)(4,1)S(1)}, s32[]{:S(2)}) async-start(s8[4718592]{0:T(1024)(128)(4,1)} %bitcast.89), calls=%async_computation.10 | async-start | bytes 1048576
  142.2 100.4 %slice-start.4 = ((s8[4718592]{0:T(1024)(128)(4,1)}), s8[524288]{0:T(1024)(128)(4,1)S(1)}, s32[]{:S(2)}) async-start(s8[4718592]{0:T(1024)(128)(4,1)} %bitcast.87), calls=%async_computation.7 | async-start | bytes 1048576
  162.7 79.9 %slice-start.5 = ((s8[4718592]{0:T(1024)(128)(4,1)}), s8[4194304]{0:T(1024)(128)(4,1)S(1)}, s32[]{:S(2)}) async-start(s8[4718592]{0:T(1024)(128)(4,1)} %bitcast.87), calls=%async_computation.8 | async-start | bytes 8388608
  242.7 103.1 %copy-start.1 = (s32[16]{0:T(128)S(1)}, s32[16]{0:T(128)}, u32[]{:S(2)}) copy-start(s32[16]{0:T(128)} %param.7) | copy-start | bytes 196
  242.7 103.1 %copy-start.3 = (f32[16,16]{0,1:T(8,128)S(1)}, f32[16,16]{0,1:T(8,128)}, u32[]{:S(2)}) copy-start(f32[16,16]{0,1:T(8,128)} %constant.146) | copy-start | bytes 3076
  242.7 123.5 %copy-start.2 = (f32[16,16]{0,1:T(8,128)S(1)}, f32[16,16]{0,1:T(8,128)}, u32[]{:S(2)}) copy-start(f32[16,16]{0,1:T(8,128)} %constant.147) | copy-start | bytes 3076
  338.7 20.6 %all-to-all-start.1 = ((f32[8,64,288]{2,1,0:T(8,128)}), f32[8,64,288]{2,1,0:T(8,128)S(1)}, u32[]{:S(2)}, u32[]{:S(2)}) async-start(f32[8,64,288]{2,1,0:T(8,128)} %bitcast.7), calls=%async_computation.1 | async-start | bytes 1572864 | tf_op jit(solution)/shard_map/all_to_all | solution.py:21
  360.1 12.1 %all-to-all-start.2 = ((f32[16,4,288]{2,1,0:T(4,128)}), f32[16,4,288]{2,1,0:T(4,128)S(1)}, u32[]{:S(2)}, u32[]{:S(2)}) async-start(f32[16,4,288]{2,1,0:T(4,128)} %reshape.87), calls=%async_computation.2 | async-start | bytes 196608 | tf_op jit(solution)/shard_map/all_to_all | solution.py:21
